TPU v7x, 32 devices: a whole 2x2x4 slice. The times are simulated.
32 devices in a mesh: mem: 8 (over y, x, core), patch: 4 (over z).
Axes of the slice: x: 2, y: 2, z: 4, core: 2. Of those that a mesh axis runs over, the one named last changes fastest.
Arguments:
- state: bfloat16 [1024, 16384], P('mem', 'patch'), may hold values from -6 to 6
- obs_ens: bfloat16 [1024, 8192], P('mem', 'patch'), may hold values from -6 to 6
- obs_values: float32 [8192], P('patch'), may hold values from -8 to 8
- obs_weight: float32 [8192], P('patch'), may hold values from 0.2 to 5
- counts: int32 [32], P('patch'), may hold values from 32 to 256
Outputs:
- analysis: bfloat16 [1024, 16384], P('mem', 'patch')
Inputs may be any that keep to these rules, and one draw needn't show every extreme that they name: Region r uses the first counts[r] of its 256 observations.
All inputs are finite; a program needn't handle non-finite values. Where the computation divides by a largest or mean magnitude, that divisor is 1e-20 or more.
Results may differ from a plain program's by a relative error of at most 0.0047.
Values may be sent and summed in bfloat16 or wider, within the bound.
A program may use at most 64 MiB of HBM per device.

v0:
```python
import math

import jax
import jax.numpy as jnp
from jax import lax
from jax.sharding import PartitionSpec as P

DEGREE = 7


def extended(cells, sides, width):
    for axis, dim in sides:
        count = lax.axis_size(axis)
        head = lax.slice_in_dim(cells, 0, width, axis=dim)
        tail = lax.slice_in_dim(cells, cells.shape[dim] - width, cells.shape[dim], axis=dim)
        cells = jnp.concatenate(
            [
                lax.ppermute(tail, axis, [(i, (i + 1) % count) for i in range(count)]),
                cells,
                lax.ppermute(head, axis, [((i + 1) % count, i) for i in range(count)]),
            ],
            axis=dim,
        )
    return cells


def root_curve(values):
    lifted = jnp.sqrt(1.0 + values)
    return -1.0 / (lifted * (1.0 + lifted))


def inverse_curve(values):
    return 1.0 / (1.0 + values)


def chebyshev(upper, curve):
    number = DEGREE + 1
    theta = (jnp.arange(number, dtype=jnp.float32) + 0.5) * (math.pi / number)
    nodes = upper * (jnp.cos(theta) + 1.0) * 0.5
    samples = curve(nodes)
    orders = jnp.arange(number, dtype=jnp.float32)
    table = jnp.cos(orders[:, None] * theta[None, :])
    coefs = 2.0 / number * jnp.sum(table * samples[None, :], axis=1)
    return coefs * jnp.where(orders == 0.0, 0.5, 1.0)


def clenshaw(block, matrix, coefs):
    nearer = coefs[DEGREE] * block
    farther = jnp.zeros_like(block)
    for order in range(DEGREE - 1, 0, -1):
        current = (
            coefs[order] * block
            + 2.0 * jnp.dot(nearer, matrix, precision=lax.Precision.HIGHEST)
            - farther
        )
        farther, nearer = (nearer, current)
    return coefs[0] * block + jnp.dot(nearer, matrix, precision=lax.Precision.HIGHEST) - farther


def cross_product(left, right):
    return lax.dot_general(
        left, right, (((0,), (0,)), ((), ())), preferred_element_type=jnp.float32
    )


def on_device(state, obs_ens, obs_values, obs_weight, counts):
    mem_index = lax.axis_index("mem")
    own = obs_ens.shape[1] // lax.axis_size("mem")
    half = own // 2
    values = lax.dynamic_slice_in_dim(obs_values, mem_index * own, own, 0)
    weights = lax.dynamic_slice_in_dim(obs_weight, mem_index * own, own, 0)
    count = lax.dynamic_slice_in_dim(counts, mem_index, 1, 0)[0]
    region_state, region_obs = (
        lax.all_to_all(state, "mem", split_axis=1, concat_axis=0, tiled=True),
        lax.all_to_all(obs_ens, "mem", split_axis=1, concat_axis=0, tiled=True),
    )
    members = region_obs.shape[0]
    full_obs = region_obs.astype(jnp.float32)
    obs_centre = jnp.mean(full_obs, axis=0)
    mask = (jnp.arange(own, dtype=jnp.int32) < count).astype(jnp.float32)
    root = jnp.sqrt(weights * mask)
    own_gains = ((full_obs - obs_centre[None, :]) * root[None, :]).astype(jnp.bfloat16)
    own_innov = (root * (values - obs_centre)).astype(jnp.bfloat16)
    stacked = jnp.concatenate([own_gains, own_innov[None, :]], axis=0)
    widened = extended(stacked, (("patch", 1),), half)
    gains = widened[:-1]
    innov = widened[-1].astype(jnp.float32)
    normal = cross_product(gains, gains) / (members - 1)
    upper = jnp.max(jnp.sum(jnp.abs(normal), axis=1)) + 1e-06
    shifted = normal * (2.0 / upper) - jnp.eye(normal.shape[0], dtype=jnp.float32)
    full = region_state.astype(jnp.float32)
    centre = jnp.mean(full, axis=0)
    spread = (full - centre[None, :]).astype(jnp.bfloat16)
    product = cross_product(spread, gains)
    mixed = clenshaw(product, shifted, chebyshev(upper, root_curve)).astype(jnp.bfloat16)
    mean_weights = clenshaw(innov[None, :], shifted, chebyshev(upper, inverse_curve))[0]
    mean_shift = jnp.dot(product, mean_weights, precision=lax.Precision.HIGHEST) / (members - 1)
    update = lax.dot_general(
        gains, mixed, (((1,), (1,)), ((), ())), preferred_element_type=jnp.float32
    ) / (members - 1)
    analysed = (full + mean_shift[None, :] + update).astype(jnp.bfloat16)
    return lax.all_to_all(analysed, "mem", split_axis=0, concat_axis=1, tiled=True)


def solution(mesh):
    placed = (P("mem", "patch"), P("mem", "patch"), P("patch"), P("patch"), P("patch"))
    return jax.shard_map(
        on_device, mesh=mesh, in_specs=placed, out_specs=P("mem", "patch"), check_vma=False
    )
```

profile of v0, /device:TPU:0, one launch (start us, length us, event | category | flops | bytes accessed | tf_op | source)
XLA Modules:
  0.0 93.4 jit_solution(3490035947268976717)
XLA Ops:
  0.0 2.1 %copy.15 = bf16[128,2048]{0,1:T(8,128)(2,1)} copy(bf16[128,2048]{1,0:T(8,128)(2,1)} %param.6) | data formatting | bytes 1048576 | tf_op args[1]
  2.1 5.2 %all-to-all-start.1 = ((bf16[128,8,256]{0,2,1:T(8,128)(2,1)}), bf16[128,8,256]{0,2,1:T(8,128)(2,1)S(1)}, u32[]{:S(2)}, u32[]{:S(2)}) async-start(bf16[128,8,256]{0,2,1:T(8,128)(2,1)} %bitcast.3), calls=%async_computation.1 | async-start | bytes 1048576 | tf_op jit(solution)/shard_map/all_to_all | solution.py:75
  7.9 9.1 %all-to-all-done.1 = bf16[128,8,256]{0,2,1:T(8,128)(2,1)S(1)} async-done(((bf16[128,8,256]{0,2,1:T(8,128)(2,1)}), bf16[128,8,256]{0,2,1:T(8,128)(2,1)S(1)}, u32[]{:S(2)}, u32[]{:S(2)}) %all-to-all-start.1) | async-done | bytes 524320 | tf_op jit(solution)/shard_map/all_to_all | solution.py:75
  17.1 1.4 %multiply_convert_fusion = (bf16[256]{0:T(256)(128)(2,1)S(1)}, f32[256]{0:T(256)S(1)}, f32[256]{0:T(256)S(1)}) fusion(f32[2048]{0:T(1024)} %param.7, s32[]{:T(128)S(6)} %select_n.15, f32[256]{0:T(256)S(1)} %convert_reduce_fusion.1, f32[2048]{0:T(1024)} %param.8, s32[]{:T(128)} %bitcast.6), kind=kLoop, calls=%fused_computation.72 | loop fusion | flops 1536 | bytes 5640 | tf_op jit(solution)/shard_map/convert_element_type | solution.py:83
  19.1 1.6 %collective-permute-start = (bf16[1025,128]{1,0:T(8,128)(2,1)S(1)}, bf16[1025,128]{1,0:T(8,128)(2,1)S(1)}, u32[]{:S(2)}, u32[]{:S(2)}) collective-permute-start(bf16[1025,128]{1,0:T(8,128)(2,1)S(1)} %get-tuple-element.11), channel_id=1, source_target_pairs={{0,1},{1,2},{2,3},{3,0},{4,5},{5,6},{6,7},{7,4},{8,9},{9,10},{10,1... | collective-permute-start | bytes 787208 | tf_op jit(solution)/shard_map/ppermute | solution.py:18
  20.8 2.2 %collective-permute-start.1 = (bf16[1025,128]{1,0:T(8,128)(2,1)S(1)}, bf16[1025,128]{1,0:T(8,128)(2,1)S(1)}, u32[]{:S(2)}, u32[]{:S(2)}) collective-permute-start(bf16[1025,128]{1,0:T(8,128)(2,1)S(1)} %get-tuple-element.12), channel_id=1, source_target_pairs={{1,0},{2,1},{3,2},{0,3},{5,4},{6,5},{7,6},{4,7},{9,8},{10,9},{11,1... | collective-permute-start | bytes 787208 | tf_op jit(solution)/shard_map/ppermute | solution.py:20
  23.0 1.1 %copy.21 = bf16[16,8,8,512]{3,2,0,1:T(8,128)(2,1)} copy(bf16[16,8,8,512]{3,2,1,0:T(8,128)(2,1)S(1)} %bitcast.86) | data formatting | bytes 2097152 | tf_op jit(solution)/shard_map/all_to_all | solution.py:74
  24.1 3.6 %all-to-all-start = ((bf16[128,8,512]{2,0,1:T(8,128)(2,1)}), bf16[128,8,512]{2,0,1:T(8,128)(2,1)S(1)}, u32[]{:S(2)}, u32[]{:S(2)}) async-start(bf16[128,8,512]{2,0,1:T(8,128)(2,1)} %bitcast.83), calls=%async_computation | async-start | bytes 2097152 | tf_op jit(solution)/shard_map/all_to_all | solution.py:74
  27.7 2.1 %collective-permute-done = bf16[1025,128]{1,0:T(8,128)(2,1)S(1)} collective-permute-done((bf16[1025,128]{1,0:T(8,128)(2,1)S(1)}, bf16[1025,128]{1,0:T(8,128)(2,1)S(1)}, u32[]{:S(2)}, u32[]{:S(2)}) %collective-permute-start) | collective-permute-done | bytes 262432 | tf_op jit(solution)/shard_map/ppermute | solution.py:18
  29.8 2.2 %collective-permute-done.1 = bf16[1025,128]{1,0:T(8,128)(2,1)S(1)} collective-permute-done((bf16[1025,128]{1,0:T(8,128)(2,1)S(1)}, bf16[1025,128]{1,0:T(8,128)(2,1)S(1)}, u32[]{:S(2)}, u32[]{:S(2)}) %collective-permute-start.1) | collective-permute-done | bytes 262432 | tf_op jit(solution)/shard_map/ppermute | solution.py:20
  36.8 4.4 %broadcast_multiply_fusion.8 = (f32[1,512]{1,0:T(1,128)S(1)}, f32[1,512]{1,0:T(1,128)S(1)}, f32[1,512]{1,0:T(1,128)S(1)}, f32[1,512]{1,0:T(1,128)S(1)}, f32[1,51...) fusion(f32[1,512]{1,0:T(1,128)S(1)} %get-tuple-element.8, f32[]{:T(128)} %bitcast.7, f32[]{:T(128)} %bitcast.19, ...), kind=kLoop, calls=%fused_computation.71 | loop fusion | flops 3584 | bytes 16412 | tf_op jit(solution)/shard_map/mul | solution.py:57
  43.1 1.0 %fusion.31 = f32[1,512]{1,0:T(1,128)S(1)} fusion(f32[512,1]{0,1:T(1,128)S(1)} %bitcast.91, f32[512,512]{0,1:T(8,128)S(1)} %get-tuple-element.38, f32[]{:T(128)S(6)} %mul.339), kind=kOutput, calls=%fused_computation.86 | convolution fusion | flops 4194304 | bytes 1052676 | tf_op jit(solution)/shard_map/dot_general | solution.py:53
  48.4 1.0 %copy-done.1 = bf16[1025,512]{1,0:T(8,128)(2,1)S(1)} copy-done((bf16[1025,512]{1,0:T(8,128)(2,1)S(1)}, bf16[1025,512]{1,0:T(8,128)(2,1)}, u32[]{:S(2)}) %copy-start.1) | copy-done | bytes 1049624
  50.2 1.0 %fusion.36 = f32[1,512]{1,0:T(1,128)S(1)} fusion(f32[512,512]{1,0:T(8,128)S(1)} %fusion.15, f32[512,1]{0,1:T(1,128)S(1)} %bitcast.96), kind=kOutput, calls=%fused_computation.90 | convolution fusion | flops 3145728 | bytes 1052672 | tf_op jit(solution)/shard_map/dot_general | solution.py:97
  51.2 3.2 %multiply_add_fusion = f32[512,512]{1,0:T(8,128)S(1)} fusion(f32[512,512]{1,0:T(8,128)S(1)} %fusion.15, f32[]{:T(128)} %bitcast.46, f32[]{:T(128)} %bitcast.45, f32[512,512]{0,1:T(8,128)S(1)} %get-tuple-element.38, f32[]{:T(128)S(6)} %mul.339), kind=kOutput, calls=%fused_computation.27 | convolution fusion | flops 1612709888 | bytes 3145740 | tf_op jit(solution)/shard_map/dot_general | solution.py:53
  54.4 1.9 %convolution_multiply_fusion.4 = f32[512,512]{1,0:T(8,128)S(1)} fusion(f32[512,512]{1,0:T(8,128)S(1)} %multiply_add_fusion, f32[512,512]{0,1:T(8,128)S(1)} %get-tuple-element.38, f32[]{:T(128)S(6)} %mul.339), kind=kOutput, calls=%fused_computation.10 | convolution fusion | flops 1611923456 | bytes 3145732 | tf_op jit(solution)/shard_map/dot_general | solution.py:53
  56.3 4.1 %add_subtract_fusion.2 = f32[512,512]{1,0:T(8,128)S(1)} fusion(f32[512,512]{1,0:T(8,128)S(1)} %multiply_add_fusion, f32[512,512]{1,0:T(8,128)S(1)} %fusion.15, f32[512,512]{1,0:T(8,128)S(1)} %convolution_multiply_fusion.4, f32[]{:T(128)} %bitcast.46, f32[]{:T(128)} %bitcast.44, f32[]{:T(128)} %bitcast.43, f32[512,512]{0,1:T(8,128)S(1)} %get-tuple-element.38, ...), kind=kOutput, calls=%fused_computation.25 | convolution fusion | flops 1613758464 | bytes 5242896 | tf_op jit(solution)/shard_map/dot_general | solution.py:53
  60.4 3.9 %add_subtract_fusion.1 = f32[512,512]{1,0:T(8,128)S(1)} fusion(f32[512,512]{1,0:T(8,128)S(1)} %fusion.15, f32[512,512]{1,0:T(8,128)S(1)} %convolution_multiply_fusion.4, f32[512,512]{1,0:T(8,128)S(1)} %add_subtract_fusion.2, f32[]{:T(128)} %bitcast.46, f32[]{:T(128)} %bitcast.44, f32[]{:T(128)} %bitcast.42, f32[512,512]{0,1:T(8,128)S(1)} %get-tuple-element.38, ...), kind=kOutput, calls=%fused_computation.24 | convolution fusion | flops 1613758464 | bytes 5242896 | tf_op jit(solution)/shard_map/dot_general | solution.py:53
  64.3 2.6 %add_subtract_fusion = f32[512,512]{1,0:T(8,128)S(1)} fusion(f32[512,512]{1,0:T(8,128)S(1)} %add_subtract_fusion.2, f32[512,512]{1,0:T(8,128)S(1)} %fusion.15, f32[512,512]{1,0:T(8,128)S(1)} %add_subtract_fusion.1, f32[]{:T(128)} %bitcast.41, f32[512,512]{0,1:T(8,128)S(1)} %get-tuple-element.38, f32[]{:T(128)S(6)} %mul.339), kind=kOutput, calls=%fused_computation.23 | convolution fusion | flops 1612709888 | bytes 5242888 | tf_op jit(solution)/shard_map/dot_general | solution.py:53
  66.9 1.9 %convolution_multiply_fusion = f32[512,512]{1,0:T(8,128)S(1)} fusion(f32[512,512]{1,0:T(8,128)S(1)} %add_subtract_fusion, f32[512,512]{0,1:T(8,128)S(1)} %get-tuple-element.38, f32[]{:T(128)S(6)} %mul.339), kind=kOutput, calls=%fused_computation.6 | convolution fusion | flops 1611923456 | bytes 3145732 | tf_op jit(solution)/shard_map/dot_general | solution.py:53
  68.8 2.6 %fusion.5 = f32[512,512]{1,0:T(8,128)S(1)} fusion(f32[512,512]{1,0:T(8,128)S(1)} %add_subtract_fusion.1, f32[512,512]{1,0:T(8,128)S(1)} %convolution_multiply_fusion, f32[512,512]{1,0:T(8,128)S(1)} %fusion.15, f32[]{:T(128)} %bitcast.40, f32[512,512]{0,1:T(8,128)S(1)} %get-tuple-element.38, f32[]{:T(128)S(6)} %mul.339), kind=kOutput, calls=%fused_computation.20 | convolution fusion | flops 1612447744 | bytes 5242888 | tf_op jit(solution)/shard_map/dot_general | solution.py:57
  71.4 1.4 %fusion.2 = bf16[1024,512]{1,0:T(8,128)(2,1)S(1)} fusion(bf16[128,8,512]{2,0,1:T(8,128)(2,1)S(1)} %all-to-all-done, f32[512]{0:T(512)S(1)} %broadcast_multiply_fusion, bf16[1025,512]{1,0:T(8,128)(2,1)S(1)} %copy-done.1, f32[512,512]{1,0:T(8,128)S(1)} %add_subtract_fusion, f32[512,512]{1,0:T(8,128)S(1)} %fusion.5, f32[512,512]{1,0:T(8,128)S(1)} %fusion.15, ...), kind=kOutput, calls=%fused_computation.5 | convolution fusion | flops 540540928 | bytes 6293508 | tf_op jit(solution)/shard_map/dot_general | solution.py:98
  72.9 19.5 %all_to_all.45 = bf16[8,128,512]{2,1,0:T(8,128)(2,1)S(1)} all-to-all(bf16[8,128,512]{2,1,0:T(8,128)(2,1)S(1)} %bitcast.85), channel_id=1, replica_groups=mesh['mem'=8,'patch'=4] {'mem'}, dimensions={0} | all-to-all | bytes 2097152 | tf_op jit(solution)/shard_map/all_to_all | solution.py:102
  92.3 1.1 %copy.19 = bf16[8,16,8,512]{3,2,0,1:T(8,128)(2,1)} copy(bf16[8,16,8,512]{3,2,1,0:T(8,128)(2,1)S(1)} %bitcast.84) | data formatting | bytes 2097152 | tf_op jit(solution)/shard_map/all_to_all | solution.py:102
  (44 shorter events, 12.4 us)
Async XLA Ops:
  0.0 7.3 %copy-start.3 = (s32[8]{0:T(128)S(1)}, s32[8]{0:T(128)}, u32[]{:S(2)}) copy-start(s32[8]{0:T(128)} %param.9) | copy-start | bytes 100
  2.1 14.9 %all-to-all-start.1 = ((bf16[128,8,256]{0,2,1:T(8,128)(2,1)}), bf16[128,8,256]{0,2,1:T(8,128)(2,1)S(1)}, u32[]{:S(2)}, u32[]{:S(2)}) async-start(bf16[128,8,256]{0,2,1:T(8,128)(2,1)} %bitcast.3), calls=%async_computation.1 | async-start | bytes 1048576 | tf_op jit(solution)/shard_map/all_to_all | solution.py:75
  19.0 4.1 %copy-start.2 = (bf16[128,4096]{1,0:T(8,128)(2,1)S(1)}, bf16[128,4096]{1,0:T(8,128)(2,1)}, u32[]{:S(2)}) copy-start(bf16[128,4096]{1,0:T(8,128)(2,1)} %param.5) | copy-start | bytes 3145732
  19.1 10.6 %collective-permute-start = (bf16[1025,128]{1,0:T(8,128)(2,1)S(1)}, bf16[1025,128]{1,0:T(8,128)(2,1)S(1)}, u32[]{:S(2)}, u32[]{:S(2)}) collective-permute-start(bf16[1025,128]{1,0:T(8,128)(2,1)S(1)} %get-tuple-element.11), channel_id=1, source_target_pairs={{0,1},{1,2},{2,3},{3,0},{4,5},{5,6},{6,7},{7,4},{8,9},{9,10},{10,1... | collective-permute-start | bytes 787208 | tf_op jit(solution)/shard_map/ppermute | solution.py:18
  20.8 11.2 %collective-permute-start.1 = (bf16[1025,128]{1,0:T(8,128)(2,1)S(1)}, bf16[1025,128]{1,0:T(8,128)(2,1)S(1)}, u32[]{:S(2)}, u32[]{:S(2)}) collective-permute-start(bf16[1025,128]{1,0:T(8,128)(2,1)S(1)} %get-tuple-element.12), channel_id=1, source_target_pairs={{1,0},{2,1},{3,2},{0,3},{5,4},{6,5},{7,6},{4,7},{9,8},{10,9},{11,1... | collective-permute-start | bytes 787208 | tf_op jit(solution)/shard_map/ppermute | solution.py:20
  24.1 23.9 %all-to-all-start = ((bf16[128,8,512]{2,0,1:T(8,128)(2,1)}), bf16[128,8,512]{2,0,1:T(8,128)(2,1)S(1)}, u32[]{:S(2)}, u32[]{:S(2)}) async-start(bf16[128,8,512]{2,0,1:T(8,128)(2,1)} %bitcast.83), calls=%async_computation | async-start | bytes 2097152 | tf_op jit(solution)/shard_map/all_to_all | solution.py:74
  32.1 1.0 %copy-start = (bf16[1025,512]{1,0:T(8,128)(2,1)}, bf16[1025,512]{1,0:T(8,128)(2,1)S(1)}, u32[]{:S(2)}) copy-start(bf16[1025,512]{1,0:T(8,128)(2,1)S(1)} %pad_maximum_fusion) | copy-start | bytes 3148804
  48.2 1.2 %copy-start.1 = (bf16[1025,512]{1,0:T(8,128)(2,1)S(1)}, bf16[1025,512]{1,0:T(8,128)(2,1)}, u32[]{:S(2)}) copy-start(bf16[1025,512]{1,0:T(8,128)(2,1)} %copy-done) | copy-start | bytes 3148804
where the time goes:
time: 94 us; the launch traced here: 93.4 us
  matrix products  30.8 us (33%)
  blocking collectives  19.5 us (21%)
  waiting for transfers between devices  13.4 us (14%)
  starting transfers between devices  12.6 us (13%)
  other arithmetic  8.41 us (9%)
  local copies, waits for them, and re-layouts  7.73 us (8%)
    dot_general x14, matrix products, clenshaw(): jnp.dot(nearer, matrix, precision=lax.Precision.HIGHEST)  26.9 us
    all_to_all x1, blocking collectives, on_device(): lax.all_to_all(analysed, 'mem', split_axis=0, concat_axis=1, tiled=True)  19.5 us
    all_to_all x1, waiting for transfers between devices, on_device(): lax.all_to_all(obs_ens, 'mem', split_axis=1, concat_axis=0, tiled=True)  9.09 us
    all_to_all x1, starting transfers between devices, on_device(): lax.all_to_all(obs_ens, 'mem', split_axis=1, concat_axis=0, tiled=True)  5.2 us
    mul x1, other arithmetic, clenshaw(): coefs[0] * block + jnp.dot(nearer, matrix, precision=lax.Precision.HIGHEST)  4.4 us
    all_to_all x1, starting transfers between devices, on_device(): lax.all_to_all(state, 'mem', split_axis=1, concat_axis=0, tiled=True)  3.56 us
    unnamed x9, local copies, waits for them, and re-layouts  3.27 us
    ppermute x1, starting transfers between devices, extended(): lax.ppermute(head, axis, [((i + 1) % count, i) for i in range(count)])  2.25 us
  transfers between devices with their start and end apart: 4, of which 3 were waited for; matrix products, arithmetic and copies ran while one was open for 18% of the time, Pallas kernels for 0%

commit v1 on v0

v1 whole, which is shorter than its diff:
```python
import functools
import math

import jax
import jax.numpy as jnp
import numpy as np
from jax import lax
from jax.experimental import pallas as pl
from jax.experimental.pallas import tpu as pltpu
from jax.sharding import PartitionSpec as P

DEGREE = 7
MESH = pl.DeviceIdType.MESH
PAD = 16


def functionals():
    number = DEGREE + 1
    theta = (np.arange(number) + 0.5) * (math.pi / number)
    rows = 2.0 / number * np.cos(np.arange(number)[:, None] * theta[None, :])
    rows[0] *= 0.5
    a = rows
    signs = np.where(np.arange(number) % 2 == 0, 1.0, -1.0)
    table = np.stack(
        [
            (signs[:, None] * a).sum(0),
            a[1] - a[7] + 2 * a[5],
            a[2] + a[6],
            a[3] - a[5] + 2 * a[7],
            a[4] - 2 * a[5] + 2 * a[6] - 2 * a[7],
            2 * a[5],
            2 * a[6],
            2 * a[7],
        ]
    )
    return (np.cos(theta) + 1.0) * 0.5, table


def flipped(index, step, count):
    bit = 1
    while bit < count:
        if step & bit:
            index = index + bit - 2 * bit * (lax.rem(index // bit, 2))
        bit *= 2
    return index


def split(row):
    high = row.astype(jnp.bfloat16)
    low = (row - high.astype(jnp.float32)).astype(jnp.bfloat16)
    return high, low


def row_times(row, matrix):
    high, low = split(row)
    k = row.shape[1]
    pick = lax.broadcasted_iota(jnp.int32, (PAD, k), 0)
    both = jnp.where(
        pick == 0,
        jnp.broadcast_to(high.astype(jnp.float32), (PAD, k)),
        jnp.where(pick == 1, jnp.broadcast_to(low.astype(jnp.float32), (PAD, k)), 0.0),
    ).astype(jnp.bfloat16)
    return jnp.sum(dot(both, matrix), axis=0, keepdims=True)


def dot(left, right):
    return jnp.dot(left, right, preferred_element_type=jnp.float32)


def kernel(
    n, npatch,
    aux_ref, obs_hbm, state_hbm, out_hbm,
    obs_v, state_v, gain, gain_t, pt, out_v,
    d1, d2, d3, d4,
    obs_ss, obs_rs, st_ss, st_rs, edge_ss, edge_rs, out_ss, out_rs, loc,
):
    me = lax.axis_index("mem")
    patch = lax.axis_index("patch")
    rows = obs_hbm.shape[0]
    own = obs_v.shape[1]
    half = own // 2
    width = state_v.shape[1]
    members = n * rows
    nobs = 2 * own
    up = lax.rem(patch + 1, npatch)
    down = lax.rem(patch + npatch - 1, npatch)

    def cols(index, size):
        return pl.ds(pl.multiple_of(index * size, size), size)

    group = max(1, 256 // rows)
    groups = n // group
    order = list(range(groups - 1, 0, -1))
    steps = [s * group + i for i in range(group) for s in order] + list(range(1, group))

    barrier = pltpu.get_barrier_semaphore()
    for s in range(1, n):
        pl.semaphore_signal(barrier, inc=1, device_id=(flipped(me, s, n), patch), device_id_type=MESH)
    for p in (up, down):
        pl.semaphore_signal(barrier, inc=1, device_id=(me, p), device_id_type=MESH)
    own_obs = pltpu.make_async_copy(obs_hbm.at[:, cols(me, own)], obs_v.at[cols(me, rows), :], loc.at[0])
    own_obs.start()
    own_state = pltpu.make_async_copy(state_hbm.at[:, cols(me, width)], state_v.at[cols(me, rows), :], loc.at[1])
    own_state.start()
    pl.semaphore_wait(barrier, n + 1)

    def obs_copy(s):
        peer = flipped(me, s, n)
        return pltpu.make_async_remote_copy(
            src_ref=obs_hbm.at[:, cols(peer, own)], dst_ref=obs_v.at[cols(me, rows), :],
            send_sem=obs_ss.at[s], recv_sem=obs_rs.at[s], device_id=(peer, patch), device_id_type=MESH)

    def state_copy(s):
        peer = flipped(me, s, n)
        return pltpu.make_async_remote_copy(
            src_ref=state_hbm.at[:, cols(peer, width)], dst_ref=state_v.at[cols(me, rows), :],
            send_sem=st_ss.at[s], recv_sem=st_rs.at[s], device_id=(peer, patch), device_id_type=MESH)

    def out_copy(s):
        peer = flipped(me, s, n)
        return pltpu.make_async_remote_copy(
            src_ref=out_v.at[cols(peer, rows), :], dst_ref=out_hbm.at[:, cols(me, width)],
            send_sem=out_ss.at[s], recv_sem=out_rs.at[s], device_id=(peer, patch), device_id_type=MESH)

    for s in steps:
        obs_copy(s).start()
    for s in steps:
        state_copy(s).start()

    own_obs.wait()
    for s in steps:
        obs_copy(s).wait_recv()
    full = obs_v[...].astype(jnp.float32)
    centre = jnp.sum(full, axis=0, keepdims=True) * (1.0 / members)
    root = aux_ref[pl.ds(me, 1), :]
    values = aux_ref[pl.ds(n + me, 1), :]
    own_gain = ((full - centre) * root).astype(jnp.bfloat16)
    innov = (root * (values - centre)).astype(jnp.bfloat16)
    for k in range(2):
        gain[k, pl.ds(0, members), :] = own_gain[:, k * half:(k + 1) * half]
        gain[k, pl.ds(members, PAD), :] = jnp.broadcast_to(
            innov[:, k * half:(k + 1) * half].astype(jnp.float32), (PAD, half)).astype(jnp.bfloat16)

    edges = [
        pltpu.make_async_remote_copy(
            src_ref=gain.at[src], dst_ref=gain.at[dst], send_sem=edge_ss.at[src], recv_sem=edge_rs.at[src],
            device_id=(me, p), device_id_type=MESH)
        for src, dst, p in ((1, 2, up), (0, 3, down))
    ]
    for e in edges:
        e.start()
    for k in range(2):
        gain_t[pl.ds(k * half, half), :] = gain[k, pl.ds(0, members), :].T
    for e in edges:
        e.wait_recv()
    for k in range(2, 4):
        gain_t[pl.ds(k * half, half), :] = gain[k, pl.ds(0, members), :].T

    def gains_of(r0, size):
        return jnp.concatenate([gain[k, pl.ds(r0, size), :] for k in range(4)], axis=1)

    normal = dot(gain_t[...], gains_of(0, members))
    upper = jnp.max(jnp.sum(jnp.abs(normal), axis=0, keepdims=True), axis=1, keepdims=True)
    upper = upper * (1.0 / (members - 1)) + 1e-06
    scaled = normal * (2.0 / (members - 1) / upper)
    d1[...] = scaled.astype(jnp.bfloat16)

    nodes, table = functionals()
    wide = jnp.broadcast_to(upper, (1, nobs))
    f_samples, e_samples = [], []
    for k in range(DEGREE + 1):
        m = wide * float(nodes[k])
        lifted = jnp.sqrt(1.0 + m)
        f_samples.append(-1.0 / (lifted * (1.0 + lifted)))
        e_samples.append(1.0 / (1.0 + m))

    def combined(samples):
        out = []
        for j in range(DEGREE + 1):
            total = samples[0] * float(table[j, 0])
            for k in range(1, DEGREE + 1):
                total = total + samples[k] * float(table[j, k])
            out.append(total)
        return out

    fa = combined(f_samples)
    ea = combined(e_samples)

    t = scaled
    second = 2.0 * dot(d1[...], d1[...]) - 4.0 * t
    d2[...] = second.astype(jnp.bfloat16)
    third = 2.0 * dot(d1[...], d2[...]) + t - 2.0 * second
    d3[...] = third.astype(jnp.bfloat16)
    fourth = 2.0 * dot(d2[...], d2[...]) + 4.0 * second
    d4[...] = fourth.astype(jnp.bfloat16)
    tail = fa[5] * t + fa[6] * second + fa[7] * third
    poly = fa[1] * t + fa[2] * second + fa[3] * third + fa[4] * fourth + dot(d4[...], tail.astype(jnp.bfloat16))

    dvec = jnp.concatenate([gain[k, pl.ds(members, PAD), :] for k in range(4)], axis=1)[0:1, :].astype(jnp.float32)
    y1 = row_times(dvec, d1[...])
    y2 = row_times(dvec, d2[...])
    y3 = row_times(dvec, d3[...])
    w = ea[5] * y1 + ea[6] * y2 + ea[7] * y3
    y4 = row_times(w + ea[4] * dvec, d4[...])
    u = ea[0] * dvec + ea[1] * y1 + ea[2] * y2 + ea[3] * y3 + y4
    poly_b = poly.astype(jnp.bfloat16)

    gsum = jnp.sum(gain_t[...].astype(jnp.float32), axis=1, keepdims=True)
    csum = jnp.zeros((1, width), jnp.float32)
    gr = group * rows
    for i, s in enumerate([0] + order[::-1]):
        base = flipped(me // group, s, groups)
        if s == 0:
            own_state.wait()
        for j in range(group):
            if s * group + j:
                state_copy(s * group + j).wait_recv()
        block = state_v[cols(base, gr), :]
        csum = csum + jnp.sum(block.astype(jnp.float32), axis=0, keepdims=True)
        part = dot(gain_t[:, cols(base, gr)], block)
        if i == 0:
            pt[...] = part
        else:
            pt[...] += part
    product = pt[...] - gsum * (csum * (1.0 / members))
    product_b = product.astype(jnp.bfloat16)
    scale = 1.0 / (members - 1)
    mixed = (fa[0][:, 0:1] * product + dot(poly_b, product_b)) * scale
    d1[...] = mixed.astype(jnp.bfloat16)
    shift = row_times(u, product_b) * scale

    for s in order + [0]:
        base = flipped(me // group, s, groups)
        start = pl.multiple_of(base * gr, gr)
        g = jnp.concatenate([gain[k, pl.ds(start, gr), :] for k in range(4)], axis=1)
        update = dot(g, d1[...])
        out_v[cols(base, gr), :] = (
            state_v[cols(base, gr), :].astype(jnp.float32) + shift + update
        ).astype(jnp.bfloat16)
        for j in range(group):
            if s * group + j:
                out_copy(s * group + j).start()
    keep = pltpu.make_async_copy(out_v.at[cols(me, rows), :], out_hbm.at[:, cols(me, width)], loc.at[2])
    keep.start()

    for e in edges:
        e.wait_send()
    for s in range(1, n):
        obs_copy(s).wait_send()
        state_copy(s).wait_send()
    keep.wait()
    for s in range(1, n):
        out_copy(s).wait()


def on_device(n, npatch, state, obs_ens, obs_values, obs_weight, counts):
    rows = obs_ens.shape[0]
    own = obs_ens.shape[1] // n
    width = state.shape[1] // n
    members = rows * n
    nobs = 2 * own
    mask = (lax.broadcasted_iota(jnp.int32, (n, own), 1) < counts[:, None]).astype(jnp.float32)
    root = jnp.sqrt(obs_weight.reshape(n, own) * mask)
    aux = jnp.concatenate([root, obs_values.reshape(n, own)], axis=0)
    bf, f32 = jnp.bfloat16, jnp.float32
    dma = pltpu.SemaphoreType.DMA
    hbm = pl.BlockSpec(memory_space=pl.ANY)
    return pl.pallas_call(
        functools.partial(kernel, n, npatch),
        out_shape=jax.ShapeDtypeStruct(state.shape, bf),
        in_specs=[pl.BlockSpec(memory_space=pltpu.VMEM), hbm, hbm],
        out_specs=hbm,
        scratch_shapes=[
            pltpu.VMEM((members, own), bf),
            pltpu.VMEM((members, width), bf),
            pltpu.VMEM((4, members + PAD, own // 2), bf),
            pltpu.VMEM((nobs, members), bf),
            pltpu.VMEM((nobs, width), f32),
            pltpu.VMEM((members, width), bf),
            pltpu.VMEM((nobs, nobs), bf),
            pltpu.VMEM((nobs, nobs), bf),
            pltpu.VMEM((nobs, nobs), bf),
            pltpu.VMEM((nobs, nobs), bf),
            dma((n,)), dma((n,)), dma((n,)), dma((n,)),
            dma((2,)), dma((2,)), dma((n,)), dma((n,)), dma((3,)),
        ],
        compiler_params=pltpu.CompilerParams(collective_id=0, has_side_effects=True),
    )(aux, obs_ens, state)


def solution(mesh):
    placed = (P("mem", "patch"), P("mem", "patch"), P("patch"), P("patch"), P("patch"))
    body = functools.partial(on_device, mesh.shape["mem"], mesh.shape["patch"])
    return jax.shard_map(
        body, mesh=mesh, in_specs=placed, out_specs=P("mem", "patch"), check_vma=False
    )
```

time: 94 us -> 49.2 us (0.52)
  Pallas kernels: 0 us -> 44.5 us
  matrix products: 30.8 us -> 0 us
  blocking collectives: 19.5 us -> 0 us
  waiting for transfers between devices: 13.4 us -> 0 us
  starting transfers between devices: 12.6 us -> 0 us
  other arithmetic: 8.41 us -> 0.69 us
  local copies, waits for them, and re-layouts: 7.73 us -> 3.66 us
    pallas_call x0 -> x1, Pallas kernels: none -> 44.5 us  [on_device(): pl.pallas_call(functools.partial(kernel, n, npatch), out_shape=jax.ShapeD...]
    dot_general x18 -> x0, matrix products: 30.8 us -> none  [the longest x14 26.9 us: clenshaw(): jnp.dot(nearer, matrix, precision=lax.Precision.HIGHEST)]
    all_to_all x1 -> x0, blocking collectives: 19.5 us -> none  [on_device(): lax.all_to_all(analysed, 'mem', split_axis=0, concat_axis=1, tiled=True)]
    all_to_all x2 -> x0, waiting for transfers between devices: 9.1 us -> none  [the longest x1 9.09 us: on_device(): lax.all_to_all(obs_ens, 'mem', split_axis=1, concat_axis=0, tiled=True)]
    all_to_all x2 -> x0, starting transfers between devices: 8.76 us -> none  [the longest x1 5.2 us: on_device(): lax.all_to_all(obs_ens, 'mem', split_axis=1, concat_axis=0, tiled=True)]
    mul x5 -> x0, other arithmetic: 5.11 us -> none  [the longest x1 4.4 us: clenshaw(): coefs[0] * block + jnp.dot(nearer, matrix, precision=lax.Precision.HIGHEST)]
    ppermute x2 -> x0, waiting for transfers between devices: 4.32 us -> none  [the longest x1 2.22 us: extended(): lax.ppermute(head, axis, [((i + 1) % count, i) for i in range(count)])]
    ppermute x2 -> x0, starting transfers between devices: 3.88 us -> none  [the longest x1 2.25 us: extended(): lax.ppermute(head, axis, [((i + 1) % count, i) for i in range(count)])]
  transfers between devices with their start and end apart: 4 -> 0, of which waited for: 3 -> 0; matrix products, arithmetic and copies ran while one was open for 18% -> 0% of each run, Pallas kernels for 0% -> 0%
where the time goes in v1:
time: 49.2 us; the launch traced here: 48.9 us
  Pallas kernels  44.5 us (90%)
  local copies, waits for them, and re-layouts  3.66 us (7%)
  other arithmetic  0.69 us (1%)
    pallas_call x1, Pallas kernels, on_device(): pl.pallas_call(functools.partial(kernel, n, npatch), out_shape=jax.ShapeD...  44.5 us
    unnamed x5, local copies, waits for them, and re-layouts  2.94 us

profile of v1, /device:TPU:0, one launch (start us, length us, event | category | flops | bytes accessed | tf_op | source)
XLA Modules:
  0.0 48.9 jit_solution(13716716163016574129)
XLA Ops:
  0.0 0.0 copy-start
  0.0 0.7 %reshape.8 = f32[8,256]{1,0:T(8,128)S(1)} reshape(f32[2048]{0:T(1024)} %param.7) | data formatting | bytes 16384 | tf_op jit(solution)/shard_map/reshape | solution.py:264
  0.7 0.0 copy-done
  0.7 0.0 copy-start.1
  0.7 0.6 %copy-done.1 = s32[8]{0:T(128)S(1)} copy-done((s32[8]{0:T(128)S(1)}, s32[8]{0:T(128)}, u32[]{:S(2)}) %copy-start.1) | copy-done | bytes 56
  1.4 0.1 select_sqrt_fusion
  1.4 0.6 %pad_maximum_fusion.aux_ref = f32[16,256]{1,0:T(8,128)} fusion(f32[8,256]{1,0:T(8,128)S(1)} %reshape.8, f32[8,256]{1,0:T(8,128)S(1)} %select_sqrt_fusion), kind=kLoop, calls=%fused_computation | loop fusion | flops 4096 | bytes 32768 | tf_op jit(solution)/shard_map/concatenate | solution.py:264
  2.1 44.5 %shard_map.55 = bf16[128,4096]{1,0:T(8,128)(2,1)} custom-call(f32[16,256]{1,0:T(8,128)} %pad_maximum_fusion.aux_ref, bf16[128,2048]{1,0:T(8,128)(2,1)} %obs_hbm.1, bf16[128,4096]{1,0:T(8,128)(2,1)} %state_hbm.1), custom_call_target="tpu_custom_call" | custom-call | tf_op jit(solution)/shard_map/pallas_call | solution.py:268
  46.6 2.3 %copy.7 = bf16[128,4096]{1,0:T(8,128)(2,1)} copy(bf16[128,4096]{1,0:T(8,128)(2,1)} %shard_map.55) | data formatting | bytes 2097152
  (1 shorter events, 0.0 us)
Async XLA Ops:
  0.0 0.7 %copy-start = (f32[2048]{0:T(1024)S(1)}, f32[2048]{0:T(1024)}, u32[]{:S(2)}) copy-start(f32[2048]{0:T(1024)} %param.8) | copy-start | bytes 24580
  0.7 0.7 %copy-start.1 = (s32[8]{0:T(128)S(1)}, s32[8]{0:T(128)}, u32[]{:S(2)}) copy-start(s32[8]{0:T(128)} %param.9) | copy-start | bytes 100

commit v2 on v1

--- a/solution.py
+++ b/solution.py
@@ -69,10 +69,10 @@
 
 def kernel(
     n, npatch,
-    aux_ref, obs_hbm, state_hbm, out_hbm,
-    obs_v, state_v, gain, gain_t, pt, out_v,
+    val_hbm, wgt_hbm, cnt_hbm, obs_hbm, state_hbm, out_hbm,
+    val_v, wgt_v, cnt_s, side, edge_v, obs_v, state_v, gain, gain_t, pt, out_v,
     d1, d2, d3, d4,
-    obs_ss, obs_rs, st_ss, st_rs, edge_ss, edge_rs, out_ss, out_rs, loc,
+    obs_ss, obs_rs, st_ss, st_rs, edge_ss, edge_rs, side_ss, side_rs, out_ss, out_rs, loc,
 ):
     me = lax.axis_index("mem")
     patch = lax.axis_index("patch")
@@ -93,6 +93,8 @@
     order = list(range(groups - 1, 0, -1))
     steps = [s * group + i for i in range(group) for s in order] + list(range(1, group))
 
+    arrivals = list(range(1, group)) + [s for s in steps if s >= group]
+
     barrier = pltpu.get_barrier_semaphore()
     for s in range(1, n):
         pl.semaphore_signal(barrier, inc=1, device_id=(flipped(me, s, n), patch), device_id_type=MESH)
@@ -102,6 +104,12 @@
     own_obs.start()
     own_state = pltpu.make_async_copy(state_hbm.at[:, cols(me, width)], state_v.at[cols(me, rows), :], loc.at[1])
     own_state.start()
+    small = [
+        pltpu.make_async_copy(src, dst, loc.at[3 + i])
+        for i, (src, dst) in enumerate(((val_hbm, val_v), (wgt_hbm, wgt_v), (cnt_hbm, cnt_s)))
+    ]
+    for c in small:
+        c.start()
     pl.semaphore_wait(barrier, n + 1)
 
     def obs_copy(s):
@@ -127,34 +135,58 @@
     for s in steps:
         state_copy(s).start()
 
+    def edge_copy(slot, s):
+        block = cols(flipped(me, s, n), rows)
+        return pltpu.make_async_remote_copy(
+            src_ref=obs_v.at[block, pl.ds((1 - slot) * half, half)], dst_ref=edge_v.at[slot, block, :],
+            send_sem=edge_ss.at[slot, s], recv_sem=edge_rs.at[slot, s],
+            device_id=(me, down if slot else up), device_id_type=MESH)
+
+    def side_copy(slot):
+        return pltpu.make_async_remote_copy(
+            src_ref=side.at[1 - slot], dst_ref=side.at[2 + slot],
+            send_sem=side_ss.at[slot], recv_sem=side_rs.at[slot],
+            device_id=(me, down if slot else up), device_id_type=MESH)
+
     own_obs.wait()
-    for s in steps:
+    for slot in range(2):
+        edge_copy(slot, 0).start()
+    for c in small:
+        c.wait()
+    count = cnt_s[me]
+    for k in range(2):
+        lane = lax.broadcasted_iota(jnp.int32, (1, half), 1) + k * half
+        mask = jnp.where(lane < count, 1.0, 0.0)
+        root = jnp.sqrt(wgt_v[pl.ds(2 * me + k, 1), :] * mask)
+        pick = lax.broadcasted_iota(jnp.int32, (8, half), 0)
+        side[k] = jnp.where(pick == 0, root, val_v[pl.ds(2 * me + k, 1), :])
+    for s in arrivals:
         obs_copy(s).wait_recv()
-    full = obs_v[...].astype(jnp.float32)
-    centre = jnp.sum(full, axis=0, keepdims=True) * (1.0 / members)
-    root = aux_ref[pl.ds(me, 1), :]
-    values = aux_ref[pl.ds(n + me, 1), :]
-    own_gain = ((full - centre) * root).astype(jnp.bfloat16)
-    innov = (root * (values - centre)).astype(jnp.bfloat16)
+        for slot in range(2):
+            edge_copy(slot, s).start()
+    for slot in range(2):
+        side_copy(slot).start()
+
+    innovs = [None] * 4
+
+    def perturb(k, block):
+        full = block.astype(jnp.float32)
+        centre = jnp.sum(full, axis=0, keepdims=True) * (1.0 / members)
+        root = side[k, pl.ds(0, 1), :]
+        values = side[k, pl.ds(1, 1), :]
+        scaled_block = ((full - centre) * root).astype(jnp.bfloat16)
+        gain[k] = scaled_block
+        gain_t[pl.ds(k * half, half), :] = scaled_block.T
+        innovs[k] = (root * (values - centre)).astype(jnp.bfloat16).astype(jnp.float32)
+
     for k in range(2):
-        gain[k, pl.ds(0, members), :] = own_gain[:, k * half:(k + 1) * half]
-        gain[k, pl.ds(members, PAD), :] = jnp.broadcast_to(
-            innov[:, k * half:(k + 1) * half].astype(jnp.float32), (PAD, half)).astype(jnp.bfloat16)
-
-    edges = [
-        pltpu.make_async_remote_copy(
-            src_ref=gain.at[src], dst_ref=gain.at[dst], send_sem=edge_ss.at[src], recv_sem=edge_rs.at[src],
-            device_id=(me, p), device_id_type=MESH)
-        for src, dst, p in ((1, 2, up), (0, 3, down))
-    ]
-    for e in edges:
-        e.start()
-    for k in range(2):
-        gain_t[pl.ds(k * half, half), :] = gain[k, pl.ds(0, members), :].T
-    for e in edges:
-        e.wait_recv()
-    for k in range(2, 4):
-        gain_t[pl.ds(k * half, half), :] = gain[k, pl.ds(0, members), :].T
+        perturb(k, obs_v[:, k * half:(k + 1) * half])
+    for slot in range(2):
+        side_copy(slot).wait_recv()
+        for s in range(n):
+            edge_copy(slot, s).wait_recv()
+    for slot in range(2):
+        perturb(2 + slot, edge_v[slot])
 
     def gains_of(r0, size):
         return jnp.concatenate([gain[k, pl.ds(r0, size), :] for k in range(4)], axis=1)
@@ -196,7 +228,7 @@
     tail = fa[5] * t + fa[6] * second + fa[7] * third
     poly = fa[1] * t + fa[2] * second + fa[3] * third + fa[4] * fourth + dot(d4[...], tail.astype(jnp.bfloat16))
 
-    dvec = jnp.concatenate([gain[k, pl.ds(members, PAD), :] for k in range(4)], axis=1)[0:1, :].astype(jnp.float32)
+    dvec = jnp.concatenate(innovs, axis=1)
     y1 = row_times(dvec, d1[...])
     y2 = row_times(dvec, d2[...])
     y3 = row_times(dvec, d3[...])
@@ -243,8 +275,10 @@
     keep = pltpu.make_async_copy(out_v.at[cols(me, rows), :], out_hbm.at[:, cols(me, width)], loc.at[2])
     keep.start()
 
-    for e in edges:
-        e.wait_send()
+    for slot in range(2):
+        side_copy(slot).wait_send()
+        for s in range(n):
+            edge_copy(slot, s).wait_send()
     for s in range(1, n):
         obs_copy(s).wait_send()
         state_copy(s).wait_send()
@@ -259,21 +293,24 @@
     width = state.shape[1] // n
     members = rows * n
     nobs = 2 * own
-    mask = (lax.broadcasted_iota(jnp.int32, (n, own), 1) < counts[:, None]).astype(jnp.float32)
-    root = jnp.sqrt(obs_weight.reshape(n, own) * mask)
-    aux = jnp.concatenate([root, obs_values.reshape(n, own)], axis=0)
+    half = own // 2
     bf, f32 = jnp.bfloat16, jnp.float32
     dma = pltpu.SemaphoreType.DMA
     hbm = pl.BlockSpec(memory_space=pl.ANY)
     return pl.pallas_call(
         functools.partial(kernel, n, npatch),
         out_shape=jax.ShapeDtypeStruct(state.shape, bf),
-        in_specs=[pl.BlockSpec(memory_space=pltpu.VMEM), hbm, hbm],
+        in_specs=[pl.BlockSpec(memory_space=pltpu.HBM)] * 5,
         out_specs=hbm,
         scratch_shapes=[
+            pltpu.VMEM((2 * n, half), f32),
+            pltpu.VMEM((2 * n, half), f32),
+            pltpu.SMEM((n,), jnp.int32),
+            pltpu.VMEM((4, 8, half), f32),
+            pltpu.VMEM((2, members, half), bf),
             pltpu.VMEM((members, own), bf),
             pltpu.VMEM((members, width), bf),
-            pltpu.VMEM((4, members + PAD, own // 2), bf),
+            pltpu.VMEM((4, members, half), bf),
             pltpu.VMEM((nobs, members), bf),
             pltpu.VMEM((nobs, width), f32),
             pltpu.VMEM((members, width), bf),
@@ -282,10 +319,10 @@
             pltpu.VMEM((nobs, nobs), bf),
             pltpu.VMEM((nobs, nobs), bf),
             dma((n,)), dma((n,)), dma((n,)), dma((n,)),
-            dma((2,)), dma((2,)), dma((n,)), dma((n,)), dma((3,)),
+            dma((2, n)), dma((2, n)), dma((2,)), dma((2,)), dma((n,)), dma((n,)), dma((6,)),
         ],
         compiler_params=pltpu.CompilerParams(collective_id=0, has_side_effects=True),
-    )(aux, obs_ens, state)
+    )(obs_values.reshape(2 * n, half), obs_weight.reshape(2 * n, half), counts, obs_ens, state)
 
 
 def solution(mesh):

time: 49.2 us -> 42 us (0.85)
  Pallas kernels: 44.5 us -> 39.6 us
  local copies, waits for them, and re-layouts: 3.66 us -> 2.29 us
  other arithmetic: 0.69 us -> 0 us
    pallas_call x1, Pallas kernels: 44.5 us -> 39.6 us  [on_device(): pl.pallas_call(functools.partial(kernel, n, npatch), out_shape=jax.ShapeD...]
    reshape x2 -> x0, local copies, waits for them, and re-layouts: 0.72 us -> none  [the longest x1 0.71 us: on_device(): aux = jnp.concatenate([root, obs_values.reshape(n, own)], axis=0)]
    unnamed x5 -> x1, local copies, waits for them, and re-layouts: 2.94 us -> 2.29 us
    concatenate x1 -> x0, other arithmetic: 0.61 us -> none  [on_device(): aux = jnp.concatenate([root, obs_values.reshape(n, own)], axis=0)]
where the time goes in v2:
time: 42 us; the launch traced here: 41.9 us
  Pallas kernels  39.6 us (94%)
  local copies, waits for them, and re-layouts  2.29 us (5%)
    pallas_call x1, Pallas kernels, on_device(): pl.pallas_call(functools.partial(kernel, n, npatch), out_shape=jax.ShapeD...  39.6 us
    unnamed x1, local copies, waits for them, and re-layouts  2.29 us

profile of v2, /device:TPU:0, one launch (start us, length us, event | category | flops | bytes accessed | tf_op | source)
XLA Modules:
  0.0 41.9 jit_solution(13033492328397109174)
XLA Ops:
  0.0 39.6 %shard_map.55 = bf16[128,4096]{1,0:T(8,128)(2,1)} custom-call(f32[16,128]{1,0:T(8,128)} %bitcast.2, f32[16,128]{1,0:T(8,128)} %bitcast.3, s32[8]{0:T(128)} %cnt_hbm.1, bf16[128,2048]{1,0:T(8,128)(2,1)} %obs_hbm.1, bf16[128,4096]{1,0:T(8,128)(2,1)} %state_hbm.1), custom_call_target="tpu_custom_call" | custom-call | tf_op jit(solution)/shard_map/pallas_call | solution.py:300
  39.6 2.3 %copy.7 = bf16[128,4096]{1,0:T(8,128)(2,1)} copy(bf16[128,4096]{1,0:T(8,128)(2,1)} %shard_map.55) | data formatting | bytes 2097152

commit v3 on v2

--- a/solution.py
+++ b/solution.py
@@ -321,8 +321,8 @@
             dma((n,)), dma((n,)), dma((n,)), dma((n,)),
             dma((2, n)), dma((2, n)), dma((2,)), dma((2,)), dma((n,)), dma((n,)), dma((6,)),
         ],
-        compiler_params=pltpu.CompilerParams(collective_id=0, has_side_effects=True),
-    )(obs_values.reshape(2 * n, half), obs_weight.reshape(2 * n, half), counts, obs_ens, state)
+        compiler_params=pltpu.CompilerParams(collective_id=0, has_side_effects=True, vmem_limit_bytes=28 * 1024 * 1024),
+    )(*(pltpu.with_memory_space_constraint(x, pltpu.HBM) for x in (obs_values.reshape(2 * n, half), obs_weight.reshape(2 * n, half), counts, obs_ens, state)))
 
 
 def solution(mesh):

time: 42 us -> 40.6 us (0.967)
  local copies, waits for them, and re-layouts: 2.29 us -> 0.97 us
    unnamed x1, local copies, waits for them, and re-layouts: 2.29 us -> 0.97 us
where the time goes in v3:
time: 40.6 us; the launch traced here: 40.5 us
  Pallas kernels  39.5 us (97%)
  local copies, waits for them, and re-layouts  0.97 us (2%)
    pallas_call x1, Pallas kernels, on_device(): pl.pallas_call(functools.partial(kernel, n, npatch), out_shape=jax.ShapeD...  39.5 us
    unnamed x1, local copies, waits for them, and re-layouts  0.97 us

profile of v3, /device:TPU:0, one launch (start us, length us, event | category | flops | bytes accessed | tf_op | source)
XLA Modules:
  0.0 40.5 jit_solution(2794040531829788244)
XLA Ops:
  0.0 39.5 %shard_map.55 = bf16[128,4096]{1,0:T(8,128)(2,1)S(1)} custom-call(f32[16,128]{1,0:T(8,128)} %bitcast.2, f32[16,128]{1,0:T(8,128)} %bitcast.3, s32[8]{0:T(128)} %cnt_hbm.1, bf16[128,2048]{1,0:T(8,128)(2,1)} %obs_hbm.1, bf16[128,4096]{1,0:T(8,128)(2,1)} %state_hbm.1), custom_call_target="tpu_custom_call" | custom-call | tf_op jit(solution)/shard_map/pallas_call | solution.py:300
  39.5 1.0 %copy.7 = bf16[128,4096]{1,0:T(8,128)(2,1)} copy(bf16[128,4096]{1,0:T(8,128)(2,1)S(1)} %shard_map.55) | data formatting | bytes 2097152

commit v4 on v3

--- a/solution.py
+++ b/solution.py
@@ -91,7 +91,7 @@
     group = max(1, 256 // rows)
     groups = n // group
     order = list(range(groups - 1, 0, -1))
-    steps = [s * group + i for i in range(group) for s in order] + list(range(1, group))
+    steps = [s * group + i for i in range(group) for s in order[::-1]] + list(range(1, group))
 
     arrivals = list(range(1, group)) + [s for s in steps if s >= group]
 

time: 40.6 us -> 40.2 us (level)
  no operation moved by 1% of the time
where the time goes in v4:
time: 40.2 us; the launch traced here: 40.1 us
  Pallas kernels  39.1 us (97%)
  local copies, waits for them, and re-layouts  0.97 us (2%)
    pallas_call x1, Pallas kernels, on_device(): pl.pallas_call(functools.partial(kernel, n, npatch), out_shape=jax.ShapeD...  39.1 us
    unnamed x1, local copies, waits for them, and re-layouts  0.97 us

profile of v4, /device:TPU:0, one launch (start us, length us, event | category | flops | bytes accessed | tf_op | source)
XLA Modules:
  0.0 40.1 jit_solution(13643870327065066406)
XLA Ops:
  0.0 39.1 %shard_map.55 = bf16[128,4096]{1,0:T(8,128)(2,1)S(1)} custom-call(f32[16,128]{1,0:T(8,128)} %bitcast.2, f32[16,128]{1,0:T(8,128)} %bitcast.3, s32[8]{0:T(128)} %cnt_hbm.1, bf16[128,2048]{1,0:T(8,128)(2,1)} %obs_hbm.1, bf16[128,4096]{1,0:T(8,128)(2,1)} %state_hbm.1), custom_call_target="tpu_custom_call" | custom-call | tf_op jit(solution)/shard_map/pallas_call | solution.py:300
  39.1 1.0 %copy.7 = bf16[128,4096]{1,0:T(8,128)(2,1)} copy(bf16[128,4096]{1,0:T(8,128)(2,1)S(1)} %shard_map.55) | data formatting | bytes 2097152
